TPU v7x, 32 devices: a whole 2x2x4 slice. The times are simulated.
32 devices in a mesh: grp: 2 (over x), patch: 16 (over z, y, core).
Axes of the slice: x: 2, y: 2, z: 4, core: 2. Of those that a mesh axis runs over, the one named last changes fastest.
Arguments:
- displace: float32 [2, 32768, 384], P('grp', 'patch'), may hold values from -6 to 6
- velocity: float32 [2, 32768, 384], P('grp', 'patch'), may hold values from -6 to 6
- ext_force: float32 [2, 32768, 384], P('grp', 'patch'), may hold values from -6 to 6
- inv_mass: float32 [2, 32768, 128], P('grp', 'patch'), may hold values from 0.1 to 6
- thickness: float32 [2, 32768, 128], P('grp', 'patch'), may hold values from 0.5 to 2
- stiff_bands: bfloat16 [5, 384, 384], replicated, may hold values from -0.125 to 0.125
- pair_points: int32 [2, 16, 3, 1536], P('grp', 'patch'), may hold values from 0 to 6143
- pair_weights: float32 [2, 16, 3, 1536], P('grp', 'patch'), may hold values from 0.25 to 1
Outputs:
- displace_new: float32 [2, 32768, 384], P('grp', 'patch')
- velocity_new: float32 [2, 32768, 384], P('grp', 'patch')
Inputs may be any that keep to these rules, and one draw needn't show every extreme that they name: `pair_points`: entry e names the control point in row e // 3 of the sending block (rows counted within the block) and point e % 3 across the strip.
All inputs are finite; a program needn't handle non-finite values.
Results may differ from a plain program's by a relative error of at most 0.00094.
The roundings to bfloat16 on the way count: a program that leaves them out, or rounds other values in their place, can miss the bound.
Values may be sent and summed in bfloat16 or wider, within the bound.
A program may use at most 192 MiB of HBM per device.

v0:
```python
import functools

import jax
import jax.numpy as jnp
from jax import lax
from jax.experimental import pallas as pl
from jax.experimental.pallas import tpu as pltpu
from jax.sharding import PartitionSpec as P

POINTS = 128
REACH = 2
SUBSTEPS = 4
EDGE = 3
COURANT = 0.4
HALO = REACH * SUBSTEPS
BASE = 2 * HALO
LANES = 128
MESH = pl.DeviceIdType.MESH


def row_chunk(rows, most):
    tiles = rows // 8
    return 8 * max(d for d in range(1, tiles + 1) if tiles % d == 0 and 8 * d <= most)


def iota(shape, dim):
    return lax.broadcasted_iota(jnp.int32, shape, dim)


def force(src, band, thick, at, length):
    around = src[pl.ds(pl.multiple_of(at - 8, 8), length + 16), :]
    parts = [
        around[8 + b - REACH : 8 + b - REACH + length].astype(jnp.bfloat16)
        for b in range(2 * REACH + 1)
    ]
    summed = jnp.dot(
        jnp.concatenate(parts, axis=1), band[...], preferred_element_type=jnp.float32
    )
    t = thick[pl.ds(at, length), :]
    return summed * jnp.concatenate([t, t, t], axis=1)


def advance(size, src, dst, vel, vel_dst, ext, mass, at, length, inner):
    m = mass[pl.ds(at, length), :]
    moved = vel[pl.ds(at, length), :] + size * (
        jnp.concatenate([m, m, m], axis=1) * (ext[pl.ds(at, length), :] - inner)
    )
    vel_dst[pl.ds(at, length), :] = moved
    dst[pl.ds(at, length), :] = src[pl.ds(at, length), :] + size * moved


def kernel(
    n_grp,
    n_patch,
    disp_hbm,
    vel_hbm,
    ext_hbm,
    mass_hbm,
    thick_hbm,
    band_hbm,
    pts_ref,
    wts_ref,
    xb,
    vel,
    ext,
    mass,
    thick,
    size_out,
    xa,
    frc,
    band,
    table,
    sent,
    got,
    spread,
    peak,
    load_sem,
    halo_send,
    halo_recv,
    trace_send,
    trace_recv,
    far_send,
    far_recv,
    peak_send,
    peak_recv,
):
    g = lax.axis_index("grp")
    p = lax.axis_index("patch")
    rows = disp_hbm.shape[1]
    width = disp_hbm.shape[2]
    slots = pts_ref.shape[2]
    total = rows + 2 * BASE
    own = pl.ds(BASE, rows)
    has_low = p > 0
    has_high = p < n_patch - 1

    loads = [
        pltpu.make_async_copy(mass_hbm.at[0], mass.at[own], load_sem.at[0]),
        pltpu.make_async_copy(thick_hbm.at[0], thick.at[own], load_sem.at[1]),
        pltpu.make_async_copy(band_hbm, band, load_sem.at[2]),
        pltpu.make_async_copy(disp_hbm.at[0], xa.at[own], load_sem.at[3]),
        pltpu.make_async_copy(vel_hbm.at[0], vel.at[own], load_sem.at[4]),
        pltpu.make_async_copy(ext_hbm.at[0], ext.at[own], load_sem.at[5]),
    ]
    for load in loads:
        load.start()

    def halo_copy(k, up):
        source, target = ((disp_hbm, xa), (vel_hbm, vel), (mass_hbm, mass), (thick_hbm, thick))[k]
        if up:
            src = source.at[0, pl.ds(rows - HALO, HALO)]
            dst = target.at[pl.ds(BASE - HALO, HALO)]
            to = p + 1
        else:
            src = source.at[0, pl.ds(0, HALO)]
            dst = target.at[pl.ds(BASE + rows, HALO)]
            to = p - 1
        return pltpu.make_async_remote_copy(
            src_ref=src,
            dst_ref=dst,
            send_sem=halo_send.at[k, int(up)],
            recv_sem=halo_recv.at[k, int(up)],
            device_id={"grp": g, "patch": to},
            device_id_type=MESH,
        )

    @pl.when(has_high)
    def _():
        for k in range(4):
            halo_copy(k, True).start()

    @pl.when(has_low)
    def _():
        for k in range(4):
            halo_copy(k, False).start()

    for buf in (xa, xb, vel, frc, ext, mass, thick):
        zero = jnp.zeros((HALO, buf.shape[1]), jnp.float32)
        buf[pl.ds(0, HALO), :] = zero
        buf[pl.ds(total - HALO, HALO), :] = zero

    @pl.when(p == 0)
    def _():
        for buf in (xa, vel, ext, mass, thick):
            buf[pl.ds(BASE - HALO, HALO), :] = jnp.zeros((HALO, buf.shape[1]), jnp.float32)
        got[0] = jnp.zeros(got.shape[1:], jnp.float32)

    @pl.when(p == n_patch - 1)
    def _():
        for buf in (xa, vel, ext, mass, thick):
            buf[pl.ds(BASE + rows, HALO), :] = jnp.zeros((HALO, buf.shape[1]), jnp.float32)
        got[2] = jnp.zeros(got.shape[1:], jnp.float32)

    loads[0].wait()
    loads[1].wait()
    peak_rows = row_chunk(rows, 256)

    def peak_step(i, high):
        at = pl.ds(pl.multiple_of(BASE + i * peak_rows, 8), peak_rows)
        product = (mass[at, :] * thick[at, :]).reshape(peak_rows // 8, 8, LANES)
        return jnp.maximum(high, jnp.max(product, axis=0))

    peak[0] = lax.fori_loop(
        0, rows // peak_rows, peak_step, jnp.zeros((8, LANES), jnp.float32)
    )
    count = n_grp * n_patch
    me = g * n_patch + p

    def peak_start(k, carry):
        to = (me + k) % count
        pltpu.make_async_remote_copy(
            src_ref=peak.at[0],
            dst_ref=peak.at[k],
            send_sem=peak_send,
            recv_sem=peak_recv,
            device_id={"grp": to // n_patch, "patch": to % n_patch},
            device_id_type=MESH,
        ).start()
        return carry

    lax.fori_loop(1, count, peak_start, 0)

    loads[2].wait()
    loads[3].wait()

    @pl.when(has_low)
    def _():
        for k in range(4):
            halo_copy(k, True).wait_recv()

    @pl.when(has_high)
    def _():
        for k in range(4):
            halo_copy(k, False).wait_recv()

    wide_chunk = row_chunk(rows + 2 * HALO, 352)
    wide_count = (rows + 2 * HALO) // wide_chunk

    def first_force(i, carry):
        at = pl.multiple_of(HALO + i * wide_chunk, 8)
        frc[pl.ds(at, wide_chunk), :] = force(xa, band, thick, at, wide_chunk)
        return carry

    lax.fori_loop(0, wide_count, first_force, 0)
    loads[4].wait()

    blocks = rows // LANES

    def edge_mix(at, length):
        return xa[pl.ds(at, length), :] + 0.5 * (
            vel[pl.ds(at, length), :] + frc[pl.ds(at, length), :]
        )

    key = iota((16, width), 0)
    lane = iota((16, width), 1)
    pick = jnp.where(
        (key % 4 == lane // POINTS) & (key // 4 == lane % POINTS), 1.0, 0.0
    ).astype(jnp.bfloat16)

    def table_step(h, carry):
        at = pl.multiple_of(BASE + h * LANES, 8)
        mix = edge_mix(at, LANES).astype(jnp.bfloat16)
        table[pl.ds(pl.multiple_of(h * 16, 16), 16), :] = lax.dot_general(
            pick, mix, (((1,), (1,)), ((), ())), preferred_element_type=jnp.float32
        ).astype(jnp.bfloat16)
        return carry

    lax.fori_loop(0, blocks, table_step, 0)

    slot_chunk = min(512, slots)
    slot_count = slots // slot_chunk
    key_col = iota((16, slot_chunk), 0) // 4
    low_col = iota((LANES, slot_chunk), 0)
    out_row = iota((8, 16), 0) % 4
    in_key = iota((8, 16), 1)
    fold = jnp.where((in_key % 4 == out_row) & (out_row < 3), 1.0, 0.0).astype(jnp.bfloat16)

    def slot_split(j, at):
        entry = pts_ref[j, :, at]
        row = entry // EDGE
        return row // LANES, row % LANES, entry - row * EDGE

    def trace_copy(j):
        return pltpu.make_async_remote_copy(
            src_ref=sent.at[j],
            dst_ref=got.at[2 - j],
            send_sem=trace_send.at[j],
            recv_sem=trace_recv.at[2 - j],
            device_id={"grp": 1 - g, "patch": p + (j - 1)},
            device_id_type=MESH,
        )

    exists = (has_low, None, has_high)

    def guarded(cond, run):
        if cond is None:
            run()
        else:
            pl.when(cond)(run)

    for j in range(3):

        def gather_step(c, carry, j=j):
            at = pl.ds(pl.multiple_of(c * slot_chunk, LANES), slot_chunk)
            high, low, point = slot_split(j, at)
            hot = jnp.where(low_col == low, 1.0, 0.0).astype(jnp.bfloat16)
            found = jnp.dot(table[...], hot, preferred_element_type=jnp.float32)
            total_found = jnp.zeros((16, slot_chunk), jnp.float32)
            for h in range(blocks):
                total_found = jnp.where(high == h, found[h * 16 : h * 16 + 16], total_found)
            total_found = jnp.where(key_col == point, total_found, 0.0)
            sent[j, :, at] = jnp.dot(
                fold, total_found.astype(jnp.bfloat16), preferred_element_type=jnp.float32
            )
            return carry

        lax.fori_loop(0, slot_count, gather_step, 0)
        guarded(exists[j], lambda j=j: trace_copy(j).start())

    spread[...] = jnp.zeros(spread.shape, jnp.float32)
    one_row = jnp.where(iota((8, slot_chunk), 0) % 4 == 3, 1.0, 0.0)
    for j in (1, 0, 2):
        guarded(exists[j], lambda j=j: trace_copy(2 - j).wait_recv())
        present = 1.0 if exists[j] is None else jnp.where(exists[j], 1.0, 0.0)

        def spread_step(c, carry, j=j, present=present):
            at = pl.ds(pl.multiple_of(c * slot_chunk, LANES), slot_chunk)
            high, low, point = slot_split(j, at)
            weight = wts_ref[j, :, at] * present
            value = (got[j, :, at] + one_row) * weight
            value = jnp.where(key_col == point, jnp.concatenate([value, value], axis=0), 0.0)
            coarse = value.astype(jnp.bfloat16).astype(jnp.float32)
            fine = value - coarse
            pieces = [jnp.where(high == h, coarse, 0.0).astype(jnp.bfloat16) for h in range(blocks)]
            pieces += [jnp.where(high == h, fine, 0.0).astype(jnp.bfloat16) for h in range(blocks)]
            hot = jnp.where(low_col == low, 1.0, 0.0).astype(jnp.bfloat16)
            spread[...] += lax.dot_general(
                jnp.concatenate(pieces, axis=0),
                hot,
                (((1,), (1,)), ((), ())),
                preferred_element_type=jnp.float32,
            )
            return carry

        lax.fori_loop(0, slot_count, spread_step, 0)

    loads[5].wait()
    key2 = iota((LANES, 2 * width), 0)
    lane2 = iota((LANES, 2 * width), 1)
    place_key = key2 % 16
    comp = place_key % 4
    hit = comp == jnp.where(lane2 < width, lane2 // POINTS, 3)
    place = jnp.where(
        hit & (place_key // 4 == lane2 % POINTS) & (key2 < 48), 1.0, 0.0
    ).astype(jnp.bfloat16)

    def couple_step(i, carry):
        h = (i + blocks - 1) % blocks
        summed = (
            spread[pl.ds(pl.multiple_of(h * 16, 16), 16), :]
            + spread[pl.ds(pl.multiple_of((blocks + h) * 16, 16), 16), :]
        )
        first = summed.astype(jnp.bfloat16).astype(jnp.float32)
        rest = summed - first
        second = rest.astype(jnp.bfloat16).astype(jnp.float32)
        stack = jnp.concatenate(
            [first, second, rest - second, jnp.zeros((LANES - 48, LANES), jnp.float32)], axis=0
        )
        placed = jnp.dot(
            stack.T.astype(jnp.bfloat16), place, preferred_element_type=jnp.float32
        )
        at = pl.multiple_of(BASE + h * LANES, 8)
        mix = edge_mix(at, LANES)
        ext[pl.ds(at, LANES), :] += placed[:, :width] - mix * placed[:, width:]
        return carry

    def far_copy(up):
        if up:
            src, dst, to = pl.ds(BASE + rows - HALO, HALO), pl.ds(BASE - HALO, HALO), p + 1
        else:
            src, dst, to = pl.ds(BASE, HALO), pl.ds(BASE + rows, HALO), p - 1
        return pltpu.make_async_remote_copy(
            src_ref=ext.at[src],
            dst_ref=ext.at[dst],
            send_sem=far_send.at[int(up)],
            recv_sem=far_recv.at[int(up)],
            device_id={"grp": g, "patch": to},
            device_id_type=MESH,
        )

    fine_group = g == 1
    lax.fori_loop(0, 2, couple_step, 0)
    pl.when(fine_group & has_high)(lambda: far_copy(True).start())
    pl.when(fine_group & has_low)(lambda: far_copy(False).start())
    lax.fori_loop(2, blocks, couple_step, 0)

    arrived = peak.at[pl.ds(1, count - 1)]
    pltpu.make_async_copy(arrived, arrived, peak_recv).wait()
    top = jnp.max(jnp.max(peak[...], axis=0), axis=(0, 1), keepdims=True)
    base_step = COURANT * (1.0 / jnp.sqrt(top))
    size = jnp.where(g == 0, SUBSTEPS * base_step, base_step)

    pl.when(fine_group & has_low)(lambda: far_copy(True).wait_recv())
    pl.when(fine_group & has_high)(lambda: far_copy(False).wait_recv())

    def step(i, carry):
        at = pl.multiple_of(HALO + i * wide_chunk, 8)
        advance(size, xa, xb, vel, vel, ext, mass, at, wide_chunk, frc[pl.ds(at, wide_chunk), :])
        return carry

    lax.fori_loop(0, wide_count, step, 0)
    size_out[...] = jnp.broadcast_to(size, size_out.shape)

    @pl.when(has_high)
    def _():
        for k in range(4):
            halo_copy(k, True).wait_send()

    @pl.when(has_low)
    def _():
        for k in range(4):
            halo_copy(k, False).wait_send()

    for j in range(3):
        guarded(exists[j], lambda j=j: trace_copy(j).wait_send())
    pl.when(fine_group & has_high)(lambda: far_copy(True).wait_send())
    pl.when(fine_group & has_low)(lambda: far_copy(False).wait_send())
    pltpu.make_async_copy(arrived, arrived, peak_send).wait()


def steps_kernel(
    xb, vel, ext, mass, thick, size_ref, band_hbm, disp_out, vel_out, xa, xc, held, band, load_sem, out_sem
):
    g = lax.axis_index("grp")
    rows = disp_out.shape[1]
    total = rows + 2 * BASE
    wide_chunk = row_chunk(rows + 2 * HALO, 352)
    wide_count = (rows + 2 * HALO) // wide_chunk
    plain_chunk = row_chunk(rows, 256)
    plain_count = rows // plain_chunk

    def outputs(src, vel, i):
        at = pl.multiple_of(i * plain_chunk, 8)
        here = pl.ds(BASE + at, plain_chunk)
        there = pl.ds(at, plain_chunk)
        return (
            pltpu.make_async_copy(src.at[here], disp_out.at[0, there], out_sem.at[0, i]),
            pltpu.make_async_copy(vel.at[here], vel_out.at[0, there], out_sem.at[1, i]),
        )

    def put(src, vel, i):
        for copy in outputs(src, vel, i):
            copy.start()

    def drain(src, vel):
        def step(i, carry):
            for copy in outputs(src, vel, i):
                copy.wait()
            return carry

        lax.fori_loop(0, plain_count, step, 0)

    @pl.when(g == 0)
    def _():
        for i in range(plain_count):
            put(xb, vel, i)
        drain(xb, vel)

    @pl.when(g == 1)
    def _():
        load = pltpu.make_async_copy(band_hbm, band, load_sem)
        load.start()
        size = size_ref[0:1, 0:1]
        zero = jnp.zeros((HALO, xa.shape[1]), jnp.float32)
        for buf in (xa, xc):
            buf[pl.ds(0, HALO), :] = zero
            buf[pl.ds(total - HALO, HALO), :] = zero
        load.wait()
        src, dst, speed = xb, xa, vel
        for _ in range(SUBSTEPS - 2):

            def step(i, carry, src=src, dst=dst, speed=speed):
                at = pl.multiple_of(HALO + i * wide_chunk, 8)
                inner = force(src, band, thick, at, wide_chunk)
                advance(size, src, dst, speed, held, ext, mass, at, wide_chunk, inner)
                return carry

            lax.fori_loop(0, wide_count, step, 0)
            src, dst, speed = dst, (xc if dst is xa else xa), held

        def last_step(i, carry):
            at = pl.multiple_of(BASE + i * plain_chunk, 8)
            inner = force(src, band, thick, at, plain_chunk)
            advance(size, src, dst, speed, held, ext, mass, at, plain_chunk, inner)
            put(dst, held, i)
            return carry

        lax.fori_loop(0, plain_count, last_step, 0)
        drain(dst, held)


def per_device(
    n_grp,
    n_patch,
    displace,
    velocity,
    ext_force,
    inv_mass,
    thickness,
    stiff_bands,
    pair_points,
    pair_weights,
):
    rows, width = displace.shape[1:]
    slots = pair_points.shape[3]
    total = rows + 2 * BASE
    blocks = rows // LANES
    points = pair_points.reshape(3, 1, slots)
    weights = pair_weights.reshape(3, 1, slots)
    bands = stiff_bands.reshape(stiff_bands.shape[0] * width, width)
    anywhere = pl.BlockSpec(memory_space=pl.ANY)
    vmem = pl.BlockSpec(memory_space=pltpu.VMEM)
    wide = pltpu.VMEM((total, width), jnp.float32)
    slim = pltpu.VMEM((total, POINTS), jnp.float32)
    dma = pltpu.SemaphoreType.DMA
    plain_count = rows // row_chunk(rows, 256)
    wide_out = pltpu.VMEM((total, width), jnp.float32)
    slim_out = pltpu.VMEM((total, POINTS), jnp.float32)
    state = pl.pallas_call(
        functools.partial(kernel, n_grp, n_patch),
        out_shape=[wide_out] * 3 + [slim_out] * 2 + [pltpu.VMEM((8, LANES), jnp.float32)],
        in_specs=[pl.BlockSpec(memory_space=pltpu.HBM)] * 6 + [vmem] * 2,
        out_specs=[vmem] * 6,
        scratch_shapes=[
            wide,
            wide,
            pltpu.VMEM(bands.shape, jnp.bfloat16),
            pltpu.VMEM((blocks * 16, LANES), jnp.bfloat16),
            pltpu.VMEM((3, 8, slots), jnp.float32),
            pltpu.VMEM((3, 8, slots), jnp.float32),
            pltpu.VMEM((blocks * 32, LANES), jnp.float32),
            pltpu.VMEM((n_grp * n_patch, 8, LANES), jnp.float32),
            dma((6,)),
            dma((4, 2)),
            dma((4, 2)),
            dma((3,)),
            dma((3,)),
            dma((2,)),
            dma((2,)),
            dma,
            dma,
        ],
        compiler_params=pltpu.CompilerParams(
            has_side_effects=True, vmem_limit_bytes=50 * 1024 * 1024
        ),
        name="couple_step",
    )(displace, velocity, ext_force, inv_mass, thickness, bands, points, weights)
    return pl.pallas_call(
        steps_kernel,
        out_shape=[jax.ShapeDtypeStruct(displace.shape, jnp.float32)] * 2,
        in_specs=[vmem] * 6 + [anywhere],
        out_specs=[anywhere] * 2,
        scratch_shapes=[
            wide,
            wide,
            wide,
            pltpu.VMEM(bands.shape, jnp.bfloat16),
            dma,
            dma((2, plain_count)),
        ],
        compiler_params=pltpu.CompilerParams(vmem_limit_bytes=24 * 1024 * 1024),
        name="fine_steps",
    )(*state, bands)


def solution(mesh):
    return jax.shard_map(
        functools.partial(per_device, mesh.shape["grp"], mesh.shape["patch"]),
        mesh=mesh,
        in_specs=(
            P("grp", "patch", None),
            P("grp", "patch", None),
            P("grp", "patch", None),
            P("grp", "patch", None),
            P("grp", "patch", None),
            P(),
            P("grp", "patch", None, None),
            P("grp", "patch", None, None),
        ),
        out_specs=(P("grp", "patch", None), P("grp", "patch", None)),
        check_vma=False,
    )
```

profile of v0, /device:TPU:3, one launch (start us, length us, event | category | flops | bytes accessed | tf_op | source)
XLA Modules:
  0.0 52.4 jit_solution(14259951833360658662)
XLA Ops:
  0.6 0.0 copy-start
  0.6 32.1 %couple_step.1 = (f32[2080,384]{1,0:T(8,128)S(1)}, f32[2080,384]{1,0:T(8,128)S(1)}, f32[2080,384]{1,0:T(8,128)S(1)}, f32[2080,128]{1,0:T(8,128)S(1)}, f32[2080,128]{1,0:T(8,128)S(1)}, /*index=5*/f32[8,128]{1,0:T(8,128)S(1)}) custom-call(f32[1,2048,384]{2,1,0:T(8,128)} %disp_hbm.1, f32[1,2048,384]{2,1,0:T(8,128)} %vel_hbm.1, f32[1,2048,384]{2,1,0:T(8,128)} %ext_hbm.1, ...), custom_call_target="tpu_custom_call" | custom-call | tf_op jit(solution)/shard_map/couple_step/pallas_call | solution.py:489
  32.8 0.0 copy-done
  32.8 19.6 %fine_steps.1 = (f32[1,2048,384]{2,1,0:T(8,128)}, f32[1,2048,384]{2,1,0:T(8,128)}) custom-call(f32[2080,384]{1,0:T(8,128)S(1)} %get-tuple-element.8.xb, f32[2080,384]{1,0:T(8,128)S(1)} %get-tuple-element.9.vel, f32[2080,384]{1,0:T(8,128)S(1)} %get-tuple-element.10.ext, f32[2080,128]{1,0:T(8,128)S(1)} %get-tuple-element.11.mass, ...), custom_call_target="tpu_custom_call" | custom-call | tf_op jit(solution)/shard_map/fine_steps/pallas_call | solution.py:518
Async XLA Ops:
  0.6 32.1 %copy-start = (bf16[5,384,384]{2,1,0:T(8,128)(2,1)S(1)}, bf16[5,384,384]{2,1,0:T(8,128)(2,1)}, u32[]{:S(2)}) copy-start(bf16[5,384,384]{2,1,0:T(8,128)(2,1)} %param.13) | copy-start | bytes 4423684
where the time goes:
time: 53 us; the launch traced here: 52.4 us
  Pallas kernels  51.7 us (98%)
  between operations  0.66 us (1%)
    pallas_call x1, Pallas kernels, per_device(): pl.pallas_call(functools.partial(kernel, n_grp, n_patch), out_shape=[wide...  32.1 us
    pallas_call x1, Pallas kernels, per_device(): pl.pallas_call(steps_kernel, out_shape=[jax.ShapeDtypeStruct(displace.sha...  19.6 us

commit v1 on v0

v1 whole, which is shorter than its diff:
```python
import functools

import jax
import jax.numpy as jnp
from jax import lax
from jax.experimental import pallas as pl
from jax.experimental.pallas import tpu as pltpu
from jax.sharding import PartitionSpec as P

POINTS = 128
REACH = 2
SUBSTEPS = 4
EDGE = 3
COURANT = 0.4
HALO = REACH * SUBSTEPS
BASE = 2 * HALO
LANES = 128
COMPS = 3
SEG = 16
OFF = 8
INNER = 4
CODES = 32
LOW = 256
F32 = jnp.float32
BF16 = jnp.bfloat16
MESH = pl.DeviceIdType.MESH


def iota(shape, dim):
    return lax.broadcasted_iota(jnp.int32, shape, dim)


def dot(a, b):
    return jnp.dot(a, b, preferred_element_type=F32)


def dot_t(a, b):
    return lax.dot_general(a, b, (((1,), (1,)), ((), ())), preferred_element_type=F32)


def split_even(total, parts):
    base, extra = divmod(total, parts)
    sizes = [base + (i < extra) for i in range(parts)]
    return [(sum(sizes[:i]), n) for i, n in enumerate(sizes)]


def pair_force(xb, band, band_mid, first, n):
    width = xb.shape[3]
    taps = [
        xb[pl.ds(first + (r - REACH) // 2 + 1, n), r % 2].reshape(n * SEG, width)
        for r in range(2 * REACH + 2)
    ]
    lhs = jnp.concatenate(taps, axis=1)
    span = (2 * REACH + 1) * width
    low = dot(lhs[:, :span], band[:, : 2 * LANES])
    mid = dot(lhs, band_mid[...])
    high = dot(lhs[:, width:], band[:, LANES:])
    even = jnp.concatenate([low, mid[:, :LANES]], axis=1)
    odd = jnp.concatenate([mid[:, LANES:], high], axis=1)
    return even.reshape(n, SEG, width), odd.reshape(n, SEG, width)


def rows_of(ref, seg_len, j):
    return jnp.concatenate(
        [ref[pl.ds(OFF + j + half * 8 * seg_len, 8, stride=seg_len), :] for half in range(2)], axis=0
    )


def wide_rows_of(ref, seg_len, j):
    return jnp.concatenate([rows_of(ref.at[c], seg_len, j) for c in range(COMPS)], axis=1)


def three(a):
    return jnp.concatenate([a, a, a], axis=-1)


def kernel(
    n_grp,
    n_patch,
    disp_hbm,
    vel_hbm,
    ext_hbm,
    mass_hbm,
    thick_hbm,
    band_hbm,
    pts_hbm,
    wts_hbm,
    xo,
    wo,
    ao,
    co,
    xb1,
    band,
    band_mid,
    size_out,
    xs,
    vs,
    es,
    ms,
    ts,
    xb0,
    sbuf,
    dd,
    mixm,
    table,
    hot,
    place,
    pts,
    wts,
    code_ref,
    wl,
    own,
    sent,
    got,
    values,
    acc,
    far_src,
    far_dst,
    peak1,
    peak2,
    load_sem,
    halo_send,
    halo_recv,
    trace_send,
    trace_recv,
    far_send,
    far_recv,
    peak_send,
    peak_recv,
):
    g = lax.axis_index("grp")
    p = lax.axis_index("patch")
    rows = disp_hbm.shape[1]
    width = disp_hbm.shape[2]
    slots = pts_hbm.shape[3]
    total = rows + 2 * BASE
    seg_len = total // SEG
    pairs = seg_len // 2
    blocks = -(-seg_len // SEG)
    start = OFF + BASE
    own_rows = pl.ds(start, rows)
    has_low = p > 0
    has_high = p < n_patch - 1
    lanes = [pl.ds(c * LANES, LANES) for c in range(COMPS)]
    span = (2 * REACH + 1) * width

    def load(src, dst, k):
        return pltpu.make_async_copy(src, dst, load_sem.at[k])

    loads = {
        "pts": [load(pts_hbm.at[0, 0], pts, 0), load(wts_hbm.at[0, 0], wts, 1)],
        "x": [load(disp_hbm.at[0, :, lanes[c]], xs.at[c, own_rows], 2 + c) for c in range(COMPS)],
        "band": [
            load(band_hbm, band, 5),
            load(band_hbm.at[:, lanes[2]], band_mid.at[pl.ds(0, span), lanes[0]], 6),
            load(band_hbm.at[:, lanes[0]], band_mid.at[pl.ds(width, span), lanes[1]], 7),
        ],
        "t": [load(thick_hbm.at[0], ts.at[own_rows], 8)],
        "v": [load(vel_hbm.at[0, :, lanes[c]], vs.at[c, own_rows], 9 + c) for c in range(COMPS)],
        "m": [load(mass_hbm.at[0], ms.at[own_rows], 12)],
        "e": [load(ext_hbm.at[0, :, lanes[c]], es.at[c, own_rows], 13 + c) for c in range(COMPS)],
    }
    for group in loads.values():
        for copy in group:
            copy.start()

    def wait(*names):
        for name in names:
            for copy in loads[name]:
                copy.wait()

    inner = n_grp * INNER
    outer = n_patch // INNER
    mine_in = g * INNER + p % INNER
    mine_out = p // INNER

    def inner_id(k):
        to = (mine_in + k) % inner
        return {"grp": to // INNER, "patch": mine_out * INNER + to % INNER}

    def outer_id(k):
        return {"grp": g, "patch": (mine_out + k) % outer * INNER + p % INNER}

    barrier = pltpu.get_barrier_semaphore()

    def greet(device_id):
        pl.semaphore_signal(barrier, inc=1, device_id=device_id, device_id_type=MESH)

    for k in range(1, inner):
        greet(inner_id(k))
    for k in range(1, outer):
        greet(outer_id(k))

    @pl.when(has_low)
    def _():
        for to in (g, 1 - g):
            greet({"grp": to, "patch": p - 1})

    @pl.when(has_high)
    def _():
        for to in (g, 1 - g):
            greet({"grp": to, "patch": p + 1})

    def zero_rows(at, n):
        for ref in (xs, vs, es):
            for c in range(COMPS):
                ref[c, pl.ds(at, n), :] = jnp.zeros((n, LANES), F32)
        for ref in (ms, ts):
            ref[pl.ds(at, n), :] = jnp.zeros((n, LANES), F32)

    zero_rows(0, start - HALO)
    zero_rows(start + rows + HALO, start - HALO)
    pl.when(p == 0)(lambda: zero_rows(start - HALO, HALO))
    pl.when(p == n_patch - 1)(lambda: zero_rows(start + rows, HALO))
    band_mid[pl.ds(span, width), lanes[0]] = jnp.zeros((width, LANES), BF16)
    band_mid[pl.ds(0, width), lanes[1]] = jnp.zeros((width, LANES), BF16)
    for c in range(seg_len * SEG, blocks * LOW, SEG):
        mixm[pl.ds(c, SEG), :] = jnp.zeros((SEG, LANES), BF16)

    wait("pts")
    entry = pts[...]
    row = entry // EDGE
    point = entry - row * EDGE
    row = row + BASE
    seg = row // seg_len
    j_row = row - seg * seg_len
    block = j_row // SEG
    code_ref[...] = block * EDGE + point
    pts[...] = (j_row - block * SEG) * SEG + seg
    third = slots // 3
    parts = [pl.ds(q * third, third) for q in range(3)]
    low_id = iota((LOW, third), 0)
    row16 = iota((SEG, third), 0)
    exists = (has_low, None, has_high)
    for j in range(3):
        weight = jnp.zeros((SEG, third), F32)
        for q in range(3):
            low = pts[pl.ds(j, 1), parts[q]]
            hot[j, :, parts[q]] = jnp.where(low_id == low, 1.0, 0.0).astype(BF16)
            weight = jnp.where(row16 % 3 == q, wts[pl.ds(j, 1), parts[q]], weight)
        present = 1.0 if exists[j] is None else jnp.where(exists[j], 1.0, 0.0)
        wl[j] = jnp.where(row16 < 3 * COMPS, weight * present, 0.0)

    place_row = iota((LOW, width), 0) % LANES
    place_lane = iota((LOW, width), 1)
    comp_row = place_row // CODES
    code_row = place_row % CODES
    hit = (comp_row == place_lane // POINTS) & (code_row % EDGE == place_lane % POINTS)
    for h in range(blocks):
        place[h] = jnp.where(hit & (code_row // EDGE == h), 1.0, 0.0).astype(BF16)

    @pl.when(p == 0)
    def _():
        got[0] = jnp.zeros(got.shape[1:], BF16)

    @pl.when(p == n_patch - 1)
    def _():
        got[2] = jnp.zeros(got.shape[1:], BF16)

    def halo_copies(name, up):
        src = pl.ds(rows - HALO, HALO) if up else pl.ds(0, HALO)
        dst = pl.ds(start - HALO, HALO) if up else pl.ds(start + rows, HALO)
        to = p + 1 if up else p - 1
        source, target, k = {
            "x": (disp_hbm, xs, 0),
            "v": (vel_hbm, vs, 3),
            "e": (ext_hbm, es, 6),
            "m": (mass_hbm, ms, 9),
            "t": (thick_hbm, ts, 10),
        }[name]
        if name in "xve":
            refs = [(source.at[0, src, lanes[c]], target.at[c, dst]) for c in range(COMPS)]
        else:
            refs = [(source.at[0, src], target.at[dst])]
        return [
            pltpu.make_async_remote_copy(
                src_ref=a,
                dst_ref=b,
                send_sem=halo_send.at[k + i, int(up)],
                recv_sem=halo_recv.at[k + i, int(up)],
                device_id={"grp": g, "patch": to},
                device_id_type=MESH,
            )
            for i, (a, b) in enumerate(refs)
        ]

    def wait_halo(*names):
        @pl.when(has_low)
        def _():
            for name in names:
                for copy in halo_copies(name, True):
                    copy.wait_recv()

        @pl.when(has_high)
        def _():
            for name in names:
                for copy in halo_copies(name, False):
                    copy.wait_recv()

    more = 2 * has_low.astype(jnp.int32) + 2 * has_high.astype(jnp.int32)
    pl.semaphore_wait(barrier, inner + outer - 2 + more)

    @pl.when(has_high)
    def _():
        for name in "xtvme":
            for copy in halo_copies(name, True):
                copy.start()

    @pl.when(has_low)
    def _():
        for name in "xtvme":
            for copy in halo_copies(name, False):
                copy.start()

    def pack(first, n):
        for i in range(first, first + n):
            for par in range(2):
                xb0[i + 1, par] = wide_rows_of(xs, seg_len, 2 * i + par).astype(BF16)

    lane = iota((SEG, LANES), 1)

    def mix_rows(first, n):
        for i in range(first, first + n):
            for par in range(2):
                j = 2 * i + par
                thick = rows_of(ts, seg_len, j)
                mixed = []
                for c in range(COMPS):
                    f = thick * sbuf[i, par, :, lanes[c]]
                    mixed.append(
                        rows_of(xs.at[c], seg_len, j) + 0.5 * (rows_of(vs.at[c], seg_len, j) + f)
                    )
                out = jnp.where(lane < 3, mixed[0], 0.0)
                out = jnp.where((lane >= 3) & (lane < 6), pltpu.roll(mixed[1], 3, 1), out)
                out = jnp.where((lane >= 6) & (lane < 9), pltpu.roll(mixed[2], 6, 1), out)
                mixm[pl.ds(j * SEG, SEG), :] = out.astype(BF16)

    def first_force(first, n):
        even, odd = pair_force(xb0, band, band_mid, first, n)
        sbuf[pl.ds(first, n), 0] = even
        sbuf[pl.ds(first, n), 1] = odd

    chunks = split_even(pairs, 4)
    middle = (chunks[1][0] - 1, chunks[1][1] + chunks[2][1] + 2)
    wait("x", "band")
    pack(*middle)
    first_force(*chunks[1])
    first_force(*chunks[2])
    wait("t", "v", "m")
    top_rows = 256
    high = jnp.zeros((8, LANES), F32)

    def peak_step(i, high):
        at = pl.ds(pl.multiple_of(start + i * top_rows, 8), top_rows)
        product = (ms[at, :] * ts[at, :]).reshape(top_rows // 8, 8, LANES)
        return jnp.maximum(high, jnp.max(product, axis=0))

    peak1[0] = lax.fori_loop(0, rows // top_rows, peak_step, high)

    def peak_copy(ref, k, to, phase):
        return pltpu.make_async_remote_copy(
            src_ref=ref.at[0],
            dst_ref=ref.at[k],
            send_sem=peak_send.at[phase],
            recv_sem=peak_recv.at[phase],
            device_id=to,
            device_id_type=MESH,
        )

    for k in range(1, inner):
        peak_copy(peak1, k, inner_id(k), 0).start()
    wait_halo("x", "t", "v")
    pack(-1, middle[0] + 1)
    pack(sum(middle), pairs + 1 - sum(middle))
    first_force(*chunks[0])
    mix_rows(*chunks[1])
    mix_rows(*chunks[2])
    first_force(*chunks[3])
    mix_rows(*chunks[0])
    mix_rows(*chunks[3])

    arrived1 = peak1.at[pl.ds(1, inner - 1)]
    pltpu.make_async_copy(arrived1, arrived1, peak_recv.at[0]).wait()
    peak2[0] = jnp.max(peak1[...], axis=0)
    for k in range(1, outer):
        peak_copy(peak2, k, outer_id(k), 1).start()

    pick_row = iota((COMPS * CODES, LANES), 0)
    pick_lane = iota((COMPS * CODES, LANES), 1)
    comp_of = pick_row // CODES
    code_of = pick_row % CODES
    picked = (pick_lane == comp_of * EDGE + code_of % EDGE) & (pick_lane < COMPS * EDGE)
    found_table = jnp.zeros((COMPS * CODES, LOW), F32)
    for h in range(blocks):
        pick = jnp.where(picked & (code_of // EDGE == h), 1.0, 0.0).astype(BF16)
        found_table += dot_t(pick, mixm[pl.ds(h * LOW, LOW), :])
    table[...] = found_table.astype(BF16)

    def trace_copy(j):
        return pltpu.make_async_remote_copy(
            src_ref=sent.at[j],
            dst_ref=got.at[2 - j],
            send_sem=trace_send.at[j],
            recv_sem=trace_recv.at[2 - j],
            device_id={"grp": 1 - g, "patch": p + (j - 1)},
            device_id_type=MESH,
        )

    def guarded(cond, run):
        if cond is None:
            run()
        else:
            pl.when(cond)(run)

    code_id = iota((CODES, third), 0)

    for j in (0, 2, 1):
        result = jnp.zeros((SEG, third), F32)
        for q in range(3):
            found = dot(table[...], hot[j, :, parts[q]])
            mask = code_id == code_ref[pl.ds(j, 1), parts[q]]
            for c in range(COMPS):
                chosen = jnp.where(mask, found[c * CODES : (c + 1) * CODES], 0.0)
                result = jnp.where(
                    row16 == c * 3 + q, jnp.sum(chosen, axis=0, keepdims=True), result
                )
        own[j] = result
        sent[j] = result.astype(BF16)
        guarded(exists[j], lambda j=j: trace_copy(j).start())

    arrived2 = peak2.at[pl.ds(1, outer - 1)]
    pltpu.make_async_copy(arrived2, arrived2, peak_recv.at[1]).wait()
    top = jnp.max(jnp.max(peak2[...], axis=0), axis=(0, 1), keepdims=True)
    base_step = COURANT * (1.0 / jnp.sqrt(top))
    size = jnp.where(g == 0, SUBSTEPS * base_step, base_step)
    square = size * size
    wait("e")
    wait_halo("m", "e")

    def prepare(i, carry):
        for k in range(10):
            j = i * 10 + k
            at = (i * 5 + k // 2, k % 2)
            mass = square * rows_of(ms, seg_len, j)
            coef = mass * rows_of(ts, seg_len, j)
            applied = three(mass) * wide_rows_of(es, seg_len, j)
            moved = size * wide_rows_of(vs, seg_len, j) + (applied - three(coef) * sbuf[at])
            ao[at] = applied
            co[at] = coef
            dd[at] = mass
            wo[at] = moved
            xo[at] = wide_rows_of(xs, seg_len, j)
        return carry

    lax.fori_loop(0, seg_len // 10, prepare, 0)

    for step, j in enumerate((1, 0, 2)):
        guarded(exists[j], lambda j=j: trace_copy(2 - j).wait_recv())
        value = (got[j].astype(F32) - own[j]) * wl[j]
        coarse = value.astype(BF16).astype(F32)
        fine = value - coarse
        for q in range(3):
            mask = code_id == code_ref[pl.ds(j, 1), parts[q]]
            zero = jnp.zeros((CODES, third), BF16)
            stack = []
            for piece in (coarse, fine):
                for c in range(COMPS):
                    one = piece[c * 3 + q : c * 3 + q + 1]
                    stack.append(jnp.where(mask, one, 0.0).astype(BF16))
                stack.append(zero)
            values[:, parts[q]] = jnp.concatenate(stack, axis=0)
        summed = dot_t(hot[j], values[...])
        if step == 0:
            acc[...] = summed
        else:
            acc[...] += summed

    both = acc[:, :LANES] + acc[:, LANES:]
    acc[:, :LANES] = both
    first = both.astype(BF16)
    pieces = jnp.concatenate([first, (both - first.astype(F32)).astype(BF16)], axis=1)

    fine_group = g == 1

    def edge_lane_rows(first_row):
        out = []
        for k in range(HALO):
            j = (first_row + k + BASE) % seg_len
            s = (first_row + k + BASE) // seg_len
            one = acc[pl.ds((j % SEG) * SEG + s, 1), lanes[0]]
            keep = iota((1, LANES), 1) % CODES // EDGE == j // SEG
            out.append(jnp.where(keep, one, 0.0))
        return jnp.concatenate(out, axis=0)

    far_src[0] = edge_lane_rows(0)
    far_src[1] = edge_lane_rows(rows - HALO)

    def far_copy(up):
        return pltpu.make_async_remote_copy(
            src_ref=far_src.at[int(up)],
            dst_ref=far_dst.at[1 - int(up)],
            send_sem=far_send.at[int(up)],
            recv_sem=far_recv.at[int(up)],
            device_id={"grp": g, "patch": p + 1 if up else p - 1},
            device_id_type=MESH,
        )

    pl.when(jnp.logical_not(fine_group & has_low))(
        lambda: far_dst.at[0].__setitem__(..., jnp.zeros((HALO, LANES), F32))
    )
    pl.when(jnp.logical_not(fine_group & has_high))(
        lambda: far_dst.at[1].__setitem__(..., jnp.zeros((HALO, LANES), F32))
    )
    pl.when(fine_group & has_high)(lambda: far_copy(True).start())
    pl.when(fine_group & has_low)(lambda: far_copy(False).start())

    half = SEG // 2

    def finish(h):
        n = min(half, pairs - h * half)
        placed = dot(pieces[: 2 * n * SEG], place[h]).reshape(n, 2, SEG, width)
        for k in range(n):
            for par in range(2):
                at = (h * half + k, par)
                extra = three(dd[at]) * placed[k, par]
                moved = wo[at] + extra
                there = xo[at] + moved
                ao[at] = ao[at] + extra
                wo[at] = moved
                xo[at] = there
                xb1[at[0] + 1, par] = there.astype(BF16)

    for h in range(blocks):
        finish(h)

    pl.when(fine_group & has_low)(lambda: far_copy(True).wait_recv())
    pl.when(fine_group & has_high)(lambda: far_copy(False).wait_recv())
    any_place = place[0]
    for h in range(1, blocks):
        any_place = any_place + place[h]
    far = far_dst[...].reshape(2 * HALO, LANES)
    far_first = far.astype(BF16)
    far_pieces = jnp.concatenate([far_first, (far - far_first.astype(F32)).astype(BF16)], axis=1)
    far_placed = dot(far_pieces, any_place)
    seg_id = iota((SEG, width), 0)
    for side, first_row in ((0, -HALO), (1, rows)):
        for k in range(HALO):
            j = (first_row + k + BASE) % seg_len
            s = (first_row + k + BASE) // seg_len
            at = (j // 2, j % 2)
            one = far_placed[side * HALO + k : side * HALO + k + 1]
            extra = three(dd[at]) * jnp.where(seg_id == s, one, 0.0)
            there = xo[at] + extra
            ao[at] = ao[at] + extra
            wo[at] = wo[at] + extra
            xo[at] = there
            xb1[at[0] + 1, at[1]] = there.astype(BF16)
    for par in range(2):
        xb1[0, par] = pltpu.roll(xo[pairs - 1, par], 1, 0).astype(BF16)
        xb1[pairs + 1, par] = pltpu.roll(xo[0, par], SEG - 1, 0).astype(BF16)
    size_out[...] = jnp.broadcast_to(1.0 / size, size_out.shape)

    @pl.when(has_high)
    def _():
        for name in "xtvme":
            for copy in halo_copies(name, True):
                copy.wait_send()

    @pl.when(has_low)
    def _():
        for name in "xtvme":
            for copy in halo_copies(name, False):
                copy.wait_send()

    for j in range(3):
        guarded(exists[j], lambda j=j: trace_copy(j).wait_send())
    pl.when(fine_group & has_high)(lambda: far_copy(True).wait_send())
    pl.when(fine_group & has_low)(lambda: far_copy(False).wait_send())
    pltpu.make_async_copy(arrived1, arrived1, peak_send.at[0]).wait()
    pltpu.make_async_copy(arrived2, arrived2, peak_send.at[1]).wait()


def steps_kernel(
    x1, w1, a, c, xb1, band, band_mid, inverse, disp_out, vel_out, xo, wo, xb2, xs, vs, out_sem
):
    g = lax.axis_index("grp")
    rows = disp_out.shape[1]
    width = disp_out.shape[2]
    total = rows + 2 * BASE
    seg_len = total // SEG
    pairs = seg_len // 2
    scale = inverse[0:1, 0:1]

    def put(i, par, x, w):
        j = 2 * i + par
        v = w * scale
        for value, ref in ((x, xs), (v, vs)):
            for c in range(COMPS):
                for half in range(2):
                    at = pl.ds(OFF + j + half * 8 * seg_len, 8, stride=seg_len)
                    ref[c, at, :] = value[half * 8 : half * 8 + 8, c * LANES : (c + 1) * LANES]

    def drain():
        copies = []
        for k, (ref, out) in enumerate(((xs, disp_out), (vs, vel_out))):
            for c in range(COMPS):
                copies.append(
                    pltpu.make_async_copy(
                        ref.at[c, pl.ds(OFF + BASE, rows)],
                        out.at[0, :, pl.ds(c * LANES, LANES)],
                        out_sem.at[k, c],
                    )
                )
        for copy in copies:
            copy.start()
        for copy in copies:
            copy.wait()

    @pl.when(g == 0)
    def _():
        def move(i, carry):
            for par in range(2):
                put(i, par, x1[i, par], w1[i, par])
            return carry

        lax.fori_loop(0, pairs, move, 0)
        drain()

    @pl.when(g == 1)
    def _():
        cur, nxt = xb1, xb2
        src_x, src_w = x1, w1
        for k in range(SUBSTEPS - 1):
            last = k == SUBSTEPS - 2
            for first, n in split_even(pairs, 4):
                here = pl.ds(first, n)
                for par, inner in enumerate(pair_force(cur, band, band_mid, first, n)):
                    w = src_w[here, par] + a[here, par] - three(c[here, par]) * inner
                    x = src_x[here, par] + w
                    if last:
                        for i in range(n):
                            put(first + i, par, x[i], w[i])
                    else:
                        wo[here, par] = w
                        xo[here, par] = x
                        nxt[pl.ds(first + 1, n), par] = x.astype(BF16)
            if not last:
                for par in range(2):
                    nxt[0, par] = pltpu.roll(xo[pairs - 1, par], 1, 0).astype(BF16)
                    nxt[pairs + 1, par] = pltpu.roll(xo[0, par], SEG - 1, 0).astype(BF16)
            cur, nxt = nxt, cur
            src_x, src_w = xo, wo
        drain()


def per_device(
    n_grp,
    n_patch,
    displace,
    velocity,
    ext_force,
    inv_mass,
    thickness,
    stiff_bands,
    pair_points,
    pair_weights,
):
    rows, width = displace.shape[1:]
    slots = pair_points.shape[3]
    total = rows + 2 * BASE
    seg_len = total // SEG
    pairs = seg_len // 2
    blocks = -(-seg_len // SEG)
    third = slots // 3
    taps = stiff_bands.shape[0]
    bands = stiff_bands.reshape(taps * width, width)
    hbm = pl.BlockSpec(memory_space=pltpu.HBM)
    vmem = pl.BlockSpec(memory_space=pltpu.VMEM)
    dma = pltpu.SemaphoreType.DMA
    lined = total + 2 * OFF
    wide = pltpu.VMEM((COMPS, lined, LANES), F32)
    slim = pltpu.VMEM((lined, LANES), F32)
    seg_wide = pltpu.VMEM((pairs, 2, SEG, width), F32)
    seg_slim = pltpu.VMEM((pairs, 2, SEG, LANES), F32)
    seg_bf16 = pltpu.VMEM((pairs + 2, 2, SEG, width), BF16)
    state = pl.pallas_call(
        functools.partial(kernel, n_grp, n_patch),
        out_shape=[
            seg_wide,
            seg_wide,
            seg_wide,
            seg_slim,
            seg_bf16,
            pltpu.VMEM(bands.shape, BF16),
            pltpu.VMEM(((taps + 1) * width, 2 * LANES), BF16),
            pltpu.VMEM((8, LANES), F32),
        ],
        in_specs=[hbm] * 8,
        out_specs=[vmem] * 8,
        scratch_shapes=[
            wide,
            wide,
            wide,
            slim,
            slim,
            seg_bf16,
            seg_wide,
            seg_slim,
            pltpu.VMEM((blocks * LOW, LANES), BF16),
            pltpu.VMEM((COMPS * CODES, LOW), BF16),
            pltpu.VMEM((3, LOW, slots), BF16),
            pltpu.VMEM((blocks, LOW, width), BF16),
            pltpu.VMEM((3, slots), jnp.int32),
            pltpu.VMEM((3, slots), F32),
            pltpu.VMEM((3, slots), jnp.int32),
            pltpu.VMEM((3, SEG, third), F32),
            pltpu.VMEM((3, SEG, third), F32),
            pltpu.VMEM((3, SEG, third), BF16),
            pltpu.VMEM((3, SEG, third), BF16),
            pltpu.VMEM((LOW, slots), BF16),
            pltpu.VMEM((LOW, LOW), F32),
            pltpu.VMEM((2, HALO, LANES), F32),
            pltpu.VMEM((2, HALO, LANES), F32),
            pltpu.VMEM((n_grp * INNER, 8, LANES), F32),
            pltpu.VMEM((n_patch // INNER, 8, LANES), F32),
            dma((16,)),
            dma((11, 2)),
            dma((11, 2)),
            dma((3,)),
            dma((3,)),
            dma((2,)),
            dma((2,)),
            dma((2,)),
            dma((2,)),
        ],
        compiler_params=pltpu.CompilerParams(
            has_side_effects=True, collective_id=0, vmem_limit_bytes=44 * 1024 * 1024
        ),
        name="couple_step",
    )(displace, velocity, ext_force, inv_mass, thickness, bands, pair_points, pair_weights)
    return pl.pallas_call(
        steps_kernel,
        out_shape=[jax.ShapeDtypeStruct(displace.shape, F32)] * 2,
        in_specs=[vmem] * 8,
        out_specs=[hbm] * 2,
        scratch_shapes=[seg_wide, seg_wide, seg_bf16, wide, wide, dma((2, COMPS))],
        compiler_params=pltpu.CompilerParams(vmem_limit_bytes=34 * 1024 * 1024),
        name="fine_steps",
    )(*state)


def solution(mesh):
    return jax.shard_map(
        functools.partial(per_device, mesh.shape["grp"], mesh.shape["patch"]),
        mesh=mesh,
        in_specs=(
            P("grp", "patch", None),
            P("grp", "patch", None),
            P("grp", "patch", None),
            P("grp", "patch", None),
            P("grp", "patch", None),
            P(),
            P("grp", "patch", None, None),
            P("grp", "patch", None, None),
        ),
        out_specs=(P("grp", "patch", None), P("grp", "patch", None)),
        check_vma=False,
    )
```

time: 53 us -> 42 us (0.79)
  Pallas kernels: 51.7 us -> 34.7 us
  local copies, waits for them, and re-layouts: 0.01 us -> 6.24 us
    pallas_call x1, Pallas kernels: 32.1 us -> 19.5 us  [per_device(): pl.pallas_call(functools.partial(kernel, n_grp, n_patch), out_shape=[seg_...]
    unnamed x2 -> x6, local copies, waits for them, and re-layouts: 0.01 us -> 6.24 us
    pallas_call x1, Pallas kernels: 19.6 us -> 15.2 us  [per_device(): pl.pallas_call(steps_kernel, out_shape=[jax.ShapeDtypeStruct(displace.sha...]
where the time goes in v1:
time: 42 us; the launch traced here: 41.8 us
  Pallas kernels  34.7 us (83%)
  local copies, waits for them, and re-layouts  6.24 us (15%)
  between operations  0.81 us (2%)
    pallas_call x1, Pallas kernels, per_device(): pl.pallas_call(functools.partial(kernel, n_grp, n_patch), out_shape=[seg_...  19.5 us
    pallas_call x1, Pallas kernels, per_device(): pl.pallas_call(steps_kernel, out_shape=[jax.ShapeDtypeStruct(displace.sha...  15.2 us
    unnamed x6, local copies, waits for them, and re-layouts  6.24 us

profile of v1, /device:TPU:3, one launch (start us, length us, event | category | flops | bytes accessed | tf_op | source)
XLA Modules:
  0.0 41.8 jit_solution(13050091547963950672)
XLA Ops:
  0.6 1.3 %copy.10.pts_hbm = s32[1,1,3,1536]{3,2,1,0:T(4,128)} copy(s32[1,1,3,1536]{3,1,2,0:T(1,128)} %param.14) | data formatting | bytes 36864 | tf_op args[6]
  2.0 1.3 %copy.11.wts_hbm = f32[1,1,3,1536]{3,2,1,0:T(4,128)} copy(f32[1,1,3,1536]{3,1,2,0:T(1,128)} %param.15) | data formatting | bytes 36864 | tf_op args[7]
  3.3 19.5 %couple_step.1 = (f32[65,2,16,384]{3,2,1,0:T(8,128)S(1)}, f32[65,2,16,384]{3,2,1,0:T(8,128)S(1)}, f32[65,2,16,384]{3,2,1,0:T(8,128)S(1)}, f32[65,2,16,128]{3,2,1...) custom-call(f32[1,2048,384]{2,1,0:T(8,128)} %disp_hbm.1, ...), custom_call_target="tpu_custom_call" | custom-call | tf_op jit(solution)/shard_map/couple_step/pallas_call | solution.py:686
  22.9 0.0 copy-start
  22.9 1.7 %copy-done = f32[65,2,16,384]{3,2,1,0:T(8,128)} copy-done((f32[65,2,16,384]{3,2,1,0:T(8,128)}, f32[65,2,16,384]{3,2,1,0:T(8,128)S(1)}, u32[]{:S(2)}) %copy-start) | copy-done | bytes 3194904
  24.5 0.0 copy-start.1
  24.5 1.9 %copy-done.1 = f32[65,2,16,384]{3,2,1,0:T(8,128)S(1)} copy-done((f32[65,2,16,384]{3,2,1,0:T(8,128)S(1)}, f32[65,2,16,384]{3,2,1,0:T(8,128)}, u32[]{:S(2)}) %copy-start.1) | copy-done | bytes 3194904
  26.4 15.2 %fine_steps.1 = (f32[1,2048,384]{2,1,0:T(8,128)}, f32[1,2048,384]{2,1,0:T(8,128)}) custom-call(f32[65,2,16,384]{3,2,1,0:T(8,128)S(1)} %get-tuple-element.10.x1, f32[65,2,16,384]{3,2,1,0:T(8,128)S(1)} %copy-done.1, f32[65,2,16,384]{3,2,1,0:T(8,128)S(1)} %get-tuple-element.12.a, f32[65,2,16,128]{3,2,1,0:T(8,128)S(1)} %get-tuple-element.13.c, ...), custom_call_target="tpu_custom_call" | custom-call | tf_op jit(solution)/shard_map/fine_steps/pallas_call | solution.py:741
Async XLA Ops:
  22.9 1.7 %copy-start = (f32[65,2,16,384]{3,2,1,0:T(8,128)}, f32[65,2,16,384]{3,2,1,0:T(8,128)S(1)}, u32[]{:S(2)}) copy-start(f32[65,2,16,384]{3,2,1,0:T(8,128)S(1)} %get-tuple-element.11.w1) | copy-start | bytes 9584644
  24.5 1.9 %copy-start.1 = (f32[65,2,16,384]{3,2,1,0:T(8,128)S(1)}, f32[65,2,16,384]{3,2,1,0:T(8,128)}, u32[]{:S(2)}) copy-start(f32[65,2,16,384]{3,2,1,0:T(8,128)} %copy-done) | copy-start | bytes 9584644

commit v2 on v1

--- a/solution.py
+++ b/solution.py
@@ -44,12 +44,16 @@
     return [(sum(sizes[:i]), n) for i, n in enumerate(sizes)]
 
 
-def pair_force(xb, band, band_mid, first, n):
+def pair_force(xb, band, band_mid, *ranges):
     width = xb.shape[3]
-    taps = [
-        xb[pl.ds(first + (r - REACH) // 2 + 1, n), r % 2].reshape(n * SEG, width)
-        for r in range(2 * REACH + 2)
-    ]
+    taps = []
+    for r in range(2 * REACH + 2):
+        got = [
+            xb[pl.ds(first + (r - REACH) // 2 + 1, n), r % 2].reshape(n * SEG, width)
+            for first, n in ranges
+        ]
+        taps.append(got[0] if len(got) == 1 else jnp.concatenate(got, axis=0))
+    n = sum(n for _, n in ranges)
     lhs = jnp.concatenate(taps, axis=1)
     span = (2 * REACH + 1) * width
     low = dot(lhs[:, :span], band[:, : 2 * LANES])
@@ -58,6 +62,26 @@
     even = jnp.concatenate([low, mid[:, :LANES]], axis=1)
     odd = jnp.concatenate([mid[:, LANES:], high], axis=1)
     return even.reshape(n, SEG, width), odd.reshape(n, SEG, width)
+
+
+def advance(sums, src, dst, a, c, nxt, *ranges):
+    done = 0
+    for first, n in ranges:
+        here = pl.ds(first, n)
+        for par in range(2):
+            inner = sums[par][done : done + n]
+            w = src[1][here, par] + a[here, par] - three(c[here, par]) * inner
+            x = src[0][here, par] + w
+            dst[0][here, par] = x
+            dst[1][here, par] = w
+            nxt[pl.ds(first + 1, n), par] = x.astype(BF16)
+        done += n
+
+
+def row_ranges(pairs):
+    edge = (BASE + REACH) // 2
+    chunks = [(edge + first, n) for first, n in split_even(pairs - 2 * edge, 3)]
+    return edge, chunks, [(0, edge), (pairs - edge, edge)]
 
 
 def rows_of(ref, seg_len, j):
@@ -90,6 +114,7 @@
     ao,
     co,
     xb1,
+    xb2,
     band,
     band_mid,
     size_out,
@@ -105,6 +130,7 @@
     table,
     hot,
     place,
+    pts_in,
     pts,
     wts,
     code_ref,
@@ -112,7 +138,6 @@
     own,
     sent,
     got,
-    values,
     acc,
     far_src,
     far_dst,
@@ -132,7 +157,7 @@
     p = lax.axis_index("patch")
     rows = disp_hbm.shape[1]
     width = disp_hbm.shape[2]
-    slots = pts_hbm.shape[3]
+    slots = pts_hbm.shape[2]
     total = rows + 2 * BASE
     seg_len = total // SEG
     pairs = seg_len // 2
@@ -148,7 +173,7 @@
         return pltpu.make_async_copy(src, dst, load_sem.at[k])
 
     loads = {
-        "pts": [load(pts_hbm.at[0, 0], pts, 0), load(wts_hbm.at[0, 0], wts, 1)],
+        "pts": [load(pts_hbm, pts_in, 0), load(wts_hbm, wts, 1)],
         "x": [load(disp_hbm.at[0, :, lanes[c]], xs.at[c, own_rows], 2 + c) for c in range(COMPS)],
         "band": [
             load(band_hbm, band, 5),
@@ -156,13 +181,17 @@
             load(band_hbm.at[:, lanes[0]], band_mid.at[pl.ds(width, span), lanes[1]], 7),
         ],
         "t": [load(thick_hbm.at[0], ts.at[own_rows], 8)],
+        "m": [load(mass_hbm.at[0], ms.at[own_rows], 12)],
         "v": [load(vel_hbm.at[0, :, lanes[c]], vs.at[c, own_rows], 9 + c) for c in range(COMPS)],
-        "m": [load(mass_hbm.at[0], ms.at[own_rows], 12)],
         "e": [load(ext_hbm.at[0, :, lanes[c]], es.at[c, own_rows], 13 + c) for c in range(COMPS)],
     }
-    for group in loads.values():
-        for copy in group:
-            copy.start()
+
+    def begin(*names):
+        for name in names:
+            for copy in loads[name]:
+                copy.start()
+
+    begin("pts", "band", "x")
 
     def wait(*names):
         for name in names:
@@ -218,7 +247,7 @@
         mixm[pl.ds(c, SEG), :] = jnp.zeros((SEG, LANES), BF16)
 
     wait("pts")
-    entry = pts[...]
+    entry = pts_in[...].reshape(3, slots)
     row = entry // EDGE
     point = entry - row * EDGE
     row = row + BASE
@@ -237,10 +266,11 @@
         for q in range(3):
             low = pts[pl.ds(j, 1), parts[q]]
             hot[j, :, parts[q]] = jnp.where(low_id == low, 1.0, 0.0).astype(BF16)
-            weight = jnp.where(row16 % 3 == q, wts[pl.ds(j, 1), parts[q]], weight)
+            weight = jnp.where(row16 % 3 == q, wts[j, :, parts[q]], weight)
         present = 1.0 if exists[j] is None else jnp.where(exists[j], 1.0, 0.0)
         wl[j] = jnp.where(row16 < 3 * COMPS, weight * present, 0.0)
 
+    begin("t", "m", "v", "e")
     place_row = iota((LOW, width), 0) % LANES
     place_lane = iota((LOW, width), 1)
     comp_row = place_row // CODES
@@ -297,21 +327,6 @@
                 for copy in halo_copies(name, False):
                     copy.wait_recv()
 
-    more = 2 * has_low.astype(jnp.int32) + 2 * has_high.astype(jnp.int32)
-    pl.semaphore_wait(barrier, inner + outer - 2 + more)
-
-    @pl.when(has_high)
-    def _():
-        for name in "xtvme":
-            for copy in halo_copies(name, True):
-                copy.start()
-
-    @pl.when(has_low)
-    def _():
-        for name in "xtvme":
-            for copy in halo_copies(name, False):
-                copy.start()
-
     def pack(first, n):
         for i in range(first, first + n):
             for par in range(2):
@@ -335,18 +350,19 @@
                 out = jnp.where((lane >= 6) & (lane < 9), pltpu.roll(mixed[2], 6, 1), out)
                 mixm[pl.ds(j * SEG, SEG), :] = out.astype(BF16)
 
-    def first_force(first, n):
-        even, odd = pair_force(xb0, band, band_mid, first, n)
-        sbuf[pl.ds(first, n), 0] = even
-        sbuf[pl.ds(first, n), 1] = odd
-
-    chunks = split_even(pairs, 4)
-    middle = (chunks[1][0] - 1, chunks[1][1] + chunks[2][1] + 2)
+    def first_force(*ranges):
+        done = 0
+        sums = pair_force(xb0, band, band_mid, *ranges)
+        for first, n in ranges:
+            for par in range(2):
+                sbuf[pl.ds(first, n), par] = sums[par][done : done + n]
+            done += n
+
+    edge, chunks, edges = row_ranges(pairs)
     wait("x", "band")
-    pack(*middle)
-    first_force(*chunks[1])
-    first_force(*chunks[2])
-    wait("t", "v", "m")
+    pack(edge - 1, pairs - 2 * edge + 2)
+    first_force(chunks[0])
+    wait("t", "m")
     top_rows = 256
     high = jnp.zeros((8, LANES), F32)
 
@@ -367,17 +383,35 @@
             device_id_type=MESH,
         )
 
+    more = 2 * has_low.astype(jnp.int32) + 2 * has_high.astype(jnp.int32)
+    pl.semaphore_wait(barrier, inner + outer - 2 + more)
+
     for k in range(1, inner):
         peak_copy(peak1, k, inner_id(k), 0).start()
+    @pl.when(has_high)
+    def _():
+        for name in "xtvme":
+            for copy in halo_copies(name, True):
+                copy.start()
+
+    @pl.when(has_low)
+    def _():
+        for name in "xtvme":
+            for copy in halo_copies(name, False):
+                copy.start()
+
+    first_force(chunks[1])
+    wait("v")
+    first_force(chunks[2])
+    mix_rows(*chunks[0])
+    mix_rows(*chunks[1])
     wait_halo("x", "t", "v")
-    pack(-1, middle[0] + 1)
-    pack(sum(middle), pairs + 1 - sum(middle))
-    first_force(*chunks[0])
-    mix_rows(*chunks[1])
+    pack(-1, edge)
+    pack(pairs - edge + 1, edge)
+    first_force(*edges)
     mix_rows(*chunks[2])
-    first_force(*chunks[3])
-    mix_rows(*chunks[0])
-    mix_rows(*chunks[3])
+    for first, n in edges:
+        mix_rows(first, n)
 
     arrived1 = peak1.at[pl.ds(1, inner - 1)]
     pltpu.make_async_copy(arrived1, arrived1, peak_recv.at[0]).wait()
@@ -428,12 +462,6 @@
         sent[j] = result.astype(BF16)
         guarded(exists[j], lambda j=j: trace_copy(j).start())
 
-    arrived2 = peak2.at[pl.ds(1, outer - 1)]
-    pltpu.make_async_copy(arrived2, arrived2, peak_recv.at[1]).wait()
-    top = jnp.max(jnp.max(peak2[...], axis=0), axis=(0, 1), keepdims=True)
-    base_step = COURANT * (1.0 / jnp.sqrt(top))
-    size = jnp.where(g == 0, SUBSTEPS * base_step, base_step)
-    square = size * size
     wait("e")
     wait_halo("m", "e")
 
@@ -441,42 +469,39 @@
         for k in range(10):
             j = i * 10 + k
             at = (i * 5 + k // 2, k % 2)
-            mass = square * rows_of(ms, seg_len, j)
+            mass = rows_of(ms, seg_len, j)
             coef = mass * rows_of(ts, seg_len, j)
             applied = three(mass) * wide_rows_of(es, seg_len, j)
-            moved = size * wide_rows_of(vs, seg_len, j) + (applied - three(coef) * sbuf[at])
             ao[at] = applied
             co[at] = coef
             dd[at] = mass
-            wo[at] = moved
+            sbuf[at] = applied - three(coef) * sbuf[at]
+            wo[at] = wide_rows_of(vs, seg_len, j)
             xo[at] = wide_rows_of(xs, seg_len, j)
         return carry
 
     lax.fori_loop(0, seg_len // 10, prepare, 0)
 
-    for step, j in enumerate((1, 0, 2)):
+    for j in range(3):
         guarded(exists[j], lambda j=j: trace_copy(2 - j).wait_recv())
+    zero = jnp.zeros((CODES, third), BF16)
+    sums = []
+    for j in range(3):
         value = (got[j].astype(F32) - own[j]) * wl[j]
         coarse = value.astype(BF16).astype(F32)
         fine = value - coarse
         for q in range(3):
             mask = code_id == code_ref[pl.ds(j, 1), parts[q]]
-            zero = jnp.zeros((CODES, third), BF16)
             stack = []
             for piece in (coarse, fine):
                 for c in range(COMPS):
                     one = piece[c * 3 + q : c * 3 + q + 1]
                     stack.append(jnp.where(mask, one, 0.0).astype(BF16))
                 stack.append(zero)
-            values[:, parts[q]] = jnp.concatenate(stack, axis=0)
-        summed = dot_t(hot[j], values[...])
-        if step == 0:
-            acc[...] = summed
-        else:
-            acc[...] += summed
-
-    both = acc[:, :LANES] + acc[:, LANES:]
-    acc[:, :LANES] = both
+            sums.append(dot_t(hot[j, :, parts[q]], jnp.concatenate(stack, axis=0)))
+    summed = sum(sums[0::2]) + sum(sums[1::2])
+    both = summed[:, :LANES] + summed[:, LANES:]
+    acc[...] = both
     first = both.astype(BF16)
     pieces = jnp.concatenate([first, (both - first.astype(F32)).astype(BF16)], axis=1)
 
@@ -487,7 +512,7 @@
         for k in range(HALO):
             j = (first_row + k + BASE) % seg_len
             s = (first_row + k + BASE) // seg_len
-            one = acc[pl.ds((j % SEG) * SEG + s, 1), lanes[0]]
+            one = acc[pl.ds((j % SEG) * SEG + s, 1), :]
             keep = iota((1, LANES), 1) % CODES // EDGE == j // SEG
             out.append(jnp.where(keep, one, 0.0))
         return jnp.concatenate(out, axis=0)
@@ -514,6 +539,12 @@
     pl.when(fine_group & has_high)(lambda: far_copy(True).start())
     pl.when(fine_group & has_low)(lambda: far_copy(False).start())
 
+    arrived2 = peak2.at[pl.ds(1, outer - 1)]
+    pltpu.make_async_copy(arrived2, arrived2, peak_recv.at[1]).wait()
+    top = jnp.max(jnp.max(peak2[...], axis=0), axis=(0, 1), keepdims=True)
+    base_step = COURANT * (1.0 / jnp.sqrt(top))
+    size = jnp.where(g == 0, SUBSTEPS * base_step, base_step)
+    square = size * size
     half = SEG // 2
 
     def finish(h):
@@ -523,15 +554,28 @@
             for par in range(2):
                 at = (h * half + k, par)
                 extra = three(dd[at]) * placed[k, par]
-                moved = wo[at] + extra
+                moved = size * wo[at] + square * (sbuf[at] + extra)
                 there = xo[at] + moved
-                ao[at] = ao[at] + extra
+                ao[at] = square * (ao[at] + extra)
+                co[at] = square * co[at]
                 wo[at] = moved
                 xo[at] = there
                 xb1[at[0] + 1, par] = there.astype(BF16)
 
-    for h in range(blocks):
-        finish(h)
+    @pl.when(g == 0)
+    def _():
+        for h in range(blocks):
+            finish(h)
+
+    @pl.when(fine_group)
+    def _():
+        done = 0
+        for first, n in chunks:
+            ready = blocks if first + n == chunks[-1][0] + chunks[-1][1] else (first + n) // half + 1
+            for h in range(done, ready):
+                finish(h)
+            done = ready
+            advance(pair_force(xb1, band, band_mid, (first, n)), (xo, wo), (xo, wo), ao, co, xb2, (first, n))
 
     pl.when(fine_group & has_low)(lambda: far_copy(True).wait_recv())
     pl.when(fine_group & has_high)(lambda: far_copy(False).wait_recv())
@@ -549,7 +593,7 @@
             s = (first_row + k + BASE) // seg_len
             at = (j // 2, j % 2)
             one = far_placed[side * HALO + k : side * HALO + k + 1]
-            extra = three(dd[at]) * jnp.where(seg_id == s, one, 0.0)
+            extra = square * three(dd[at]) * jnp.where(seg_id == s, one, 0.0)
             there = xo[at] + extra
             ao[at] = ao[at] + extra
             wo[at] = wo[at] + extra
@@ -581,7 +625,7 @@
 
 
 def steps_kernel(
-    x1, w1, a, c, xb1, band, band_mid, inverse, disp_out, vel_out, xo, wo, xb2, xs, vs, out_sem
+    x1, w1, a, c, xb1, mids, band, band_mid, inverse, disp_out, vel_out, xo, wo, xb2, xb3, xs, vs, out_sem
 ):
     g = lax.axis_index("grp")
     rows = disp_out.shape[1]
@@ -628,28 +672,34 @@
 
     @pl.when(g == 1)
     def _():
-        cur, nxt = xb1, xb2
-        src_x, src_w = x1, w1
-        for k in range(SUBSTEPS - 1):
-            last = k == SUBSTEPS - 2
-            for first, n in split_even(pairs, 4):
-                here = pl.ds(first, n)
-                for par, inner in enumerate(pair_force(cur, band, band_mid, first, n)):
-                    w = src_w[here, par] + a[here, par] - three(c[here, par]) * inner
-                    x = src_x[here, par] + w
-                    if last:
-                        for i in range(n):
-                            put(first + i, par, x[i], w[i])
-                    else:
-                        wo[here, par] = w
-                        xo[here, par] = x
-                        nxt[pl.ds(first + 1, n), par] = x.astype(BF16)
-            if not last:
-                for par in range(2):
-                    nxt[0, par] = pltpu.roll(xo[pairs - 1, par], 1, 0).astype(BF16)
-                    nxt[pairs + 1, par] = pltpu.roll(xo[0, par], SEG - 1, 0).astype(BF16)
-            cur, nxt = nxt, cur
-            src_x, src_w = xo, wo
+        _, chunks, edges = row_ranges(pairs)
+        order = [[chunks[1]], [chunks[0]], [chunks[2]], edges]
+        middle = pl.ds(chunks[0][0] + 1, sum(n for _, n in chunks))
+
+        def wrap(nxt):
+            for par in range(2):
+                nxt[0, par] = pltpu.roll(xo[pairs - 1, par], 1, 0).astype(BF16)
+                nxt[pairs + 1, par] = pltpu.roll(xo[0, par], SEG - 1, 0).astype(BF16)
+
+        sums = pair_force(xb1, band, band_mid, *edges)
+        advance(sums, (x1, w1), (xo, wo), a, c, xb2, *edges)
+        xb2[middle] = mids[middle]
+        wrap(xb2)
+        for ranges in order:
+            src = (xo, wo) if ranges is edges else (x1, w1)
+            sums = pair_force(xb2, band, band_mid, *ranges)
+            advance(sums, src, (xo, wo), a, c, xb3, *ranges)
+        wrap(xb3)
+        for ranges in order:
+            sums = pair_force(xb3, band, band_mid, *ranges)
+            done = 0
+            for first, n in ranges:
+                for i in range(n):
+                    for par in range(2):
+                        at = (first + i, par)
+                        w = wo[at] + a[at] - three(c[at]) * sums[par][done + i]
+                        put(first + i, par, xo[at] + w, w)
+                done += n
         drain()
 
 
@@ -674,6 +724,8 @@
     third = slots // 3
     taps = stiff_bands.shape[0]
     bands = stiff_bands.reshape(taps * width, width)
+    points = pair_points.reshape(3, 1, slots)
+    weights = pair_weights.reshape(3, 1, slots)
     hbm = pl.BlockSpec(memory_space=pltpu.HBM)
     vmem = pl.BlockSpec(memory_space=pltpu.VMEM)
     dma = pltpu.SemaphoreType.DMA
@@ -691,12 +743,13 @@
             seg_wide,
             seg_slim,
             seg_bf16,
+            seg_bf16,
             pltpu.VMEM(bands.shape, BF16),
             pltpu.VMEM(((taps + 1) * width, 2 * LANES), BF16),
             pltpu.VMEM((8, LANES), F32),
         ],
         in_specs=[hbm] * 8,
-        out_specs=[vmem] * 8,
+        out_specs=[vmem] * 9,
         scratch_shapes=[
             wide,
             wide,
@@ -710,15 +763,15 @@
             pltpu.VMEM((COMPS * CODES, LOW), BF16),
             pltpu.VMEM((3, LOW, slots), BF16),
             pltpu.VMEM((blocks, LOW, width), BF16),
+            pltpu.VMEM((3, 1, slots), jnp.int32),
             pltpu.VMEM((3, slots), jnp.int32),
-            pltpu.VMEM((3, slots), F32),
+            pltpu.VMEM((3, 1, slots), F32),
             pltpu.VMEM((3, slots), jnp.int32),
             pltpu.VMEM((3, SEG, third), F32),
             pltpu.VMEM((3, SEG, third), F32),
             pltpu.VMEM((3, SEG, third), BF16),
             pltpu.VMEM((3, SEG, third), BF16),
-            pltpu.VMEM((LOW, slots), BF16),
-            pltpu.VMEM((LOW, LOW), F32),
+            pltpu.VMEM((LOW, LANES), F32),
             pltpu.VMEM((2, HALO, LANES), F32),
             pltpu.VMEM((2, HALO, LANES), F32),
             pltpu.VMEM((n_grp * INNER, 8, LANES), F32),
@@ -737,14 +790,14 @@
             has_side_effects=True, collective_id=0, vmem_limit_bytes=44 * 1024 * 1024
         ),
         name="couple_step",
-    )(displace, velocity, ext_force, inv_mass, thickness, bands, pair_points, pair_weights)
+    )(displace, velocity, ext_force, inv_mass, thickness, bands, points, weights)
     return pl.pallas_call(
         steps_kernel,
         out_shape=[jax.ShapeDtypeStruct(displace.shape, F32)] * 2,
-        in_specs=[vmem] * 8,
+        in_specs=[vmem] * 9,
         out_specs=[hbm] * 2,
-        scratch_shapes=[seg_wide, seg_wide, seg_bf16, wide, wide, dma((2, COMPS))],
-        compiler_params=pltpu.CompilerParams(vmem_limit_bytes=34 * 1024 * 1024),
+        scratch_shapes=[seg_wide, seg_wide, seg_bf16, seg_bf16, wide, wide, dma((2, COMPS))],
+        compiler_params=pltpu.CompilerParams(vmem_limit_bytes=20 * 1024 * 1024),
         name="fine_steps",
     )(*state)
 

time: 42 us -> 31.8 us (0.76)
  local copies, waits for them, and re-layouts: 6.24 us -> 0 us
  Pallas kernels: 34.7 us -> 30.9 us
    unnamed x6 -> x0, local copies, waits for them, and re-layouts: 6.24 us -> none
    pallas_call x1, Pallas kernels: 15.2 us -> 11.3 us  [per_device(): pl.pallas_call(steps_kernel, out_shape=[jax.ShapeDtypeStruct(displace.sha...]
where the time goes in v2:
time: 31.8 us; the launch traced here: 31.7 us
  Pallas kernels  30.9 us (97%)
  between operations  0.8 us (3%)
    pallas_call x1, Pallas kernels, per_device(): pl.pallas_call(functools.partial(kernel, n_grp, n_patch), out_shape=[seg_...  19.6 us
    pallas_call x1, Pallas kernels, per_device(): pl.pallas_call(steps_kernel, out_shape=[jax.ShapeDtypeStruct(displace.sha...  11.3 us

profile of v2, /device:TPU:3, one launch (start us, length us, event | category | flops | bytes accessed | tf_op | source)
XLA Modules:
  0.0 31.7 jit_solution(4710029708490260844)
XLA Ops:
  0.6 19.6 %couple_step.1 = (f32[65,2,16,384]{3,2,1,0:T(8,128)S(1)}, f32[65,2,16,384]{3,2,1,0:T(8,128)S(1)}, f32[65,2,16,384]{3,2,1,0:T(8,128)S(1)}, f32[65,2,16,128]{3,2,1...) custom-call(f32[1,2048,384]{2,1,0:T(8,128)} %disp_hbm.1, ...), custom_call_target="tpu_custom_call" | custom-call | tf_op jit(solution)/shard_map/couple_step/pallas_call | solution.py:738
  20.2 11.3 %fine_steps.1 = (f32[1,2048,384]{2,1,0:T(8,128)}, f32[1,2048,384]{2,1,0:T(8,128)}) custom-call(f32[65,2,16,384]{3,2,1,0:T(8,128)S(1)} %get-tuple-element.11.x1, f32[65,2,16,384]{3,2,1,0:T(8,128)S(1)} %get-tuple-element.12.w1, f32[65,2,16,384]{3,2,1,0:T(8,128)S(1)} %get-tuple-element.13.a, f32[65,2,16,128]{3,2,1,0:T(8,128)S(1)} %get-tuple-element.14.c, ...), custom_call_target="tpu_custom_call" | custom-call | tf_op jit(solution)/shard_map/fine_steps/pallas_call | solution.py:794

commit v3 on v2

--- a/solution.py
+++ b/solution.py
@@ -36,6 +36,10 @@
 
 def dot_t(a, b):
     return lax.dot_general(a, b, (((1,), (1,)), ((), ())), preferred_element_type=F32)
+
+
+def apart(index, a):
+    return jnp.where(index >= 0, a, 0.0)
 
 
 def split_even(total, parts):
@@ -175,11 +179,7 @@
     loads = {
         "pts": [load(pts_hbm, pts_in, 0), load(wts_hbm, wts, 1)],
         "x": [load(disp_hbm.at[0, :, lanes[c]], xs.at[c, own_rows], 2 + c) for c in range(COMPS)],
-        "band": [
-            load(band_hbm, band, 5),
-            load(band_hbm.at[:, lanes[2]], band_mid.at[pl.ds(0, span), lanes[0]], 6),
-            load(band_hbm.at[:, lanes[0]], band_mid.at[pl.ds(width, span), lanes[1]], 7),
-        ],
+        "band": [load(band_hbm, band, 5)],
         "t": [load(thick_hbm.at[0], ts.at[own_rows], 8)],
         "m": [load(mass_hbm.at[0], ms.at[own_rows], 12)],
         "v": [load(vel_hbm.at[0, :, lanes[c]], vs.at[c, own_rows], 9 + c) for c in range(COMPS)],
@@ -288,20 +288,14 @@
         got[2] = jnp.zeros(got.shape[1:], BF16)
 
     def halo_copies(name, up):
-        src = pl.ds(rows - HALO, HALO) if up else pl.ds(0, HALO)
-        dst = pl.ds(start - HALO, HALO) if up else pl.ds(start + rows, HALO)
+        src = pl.ds(start + rows - HALO if up else start, HALO)
+        dst = pl.ds(start - HALO if up else start + rows, HALO)
         to = p + 1 if up else p - 1
-        source, target, k = {
-            "x": (disp_hbm, xs, 0),
-            "v": (vel_hbm, vs, 3),
-            "e": (ext_hbm, es, 6),
-            "m": (mass_hbm, ms, 9),
-            "t": (thick_hbm, ts, 10),
-        }[name]
+        target, k = {"x": (xs, 0), "v": (vs, 3), "e": (es, 6), "m": (ms, 9), "t": (ts, 10)}[name]
         if name in "xve":
-            refs = [(source.at[0, src, lanes[c]], target.at[c, dst]) for c in range(COMPS)]
+            refs = [(target.at[c, src], target.at[c, dst]) for c in range(COMPS)]
         else:
-            refs = [(source.at[0, src], target.at[dst])]
+            refs = [(target.at[src], target.at[dst])]
         return [
             pltpu.make_async_remote_copy(
                 src_ref=a,
@@ -313,6 +307,19 @@
             )
             for i, (a, b) in enumerate(refs)
         ]
+
+    def start_halo(*names):
+        @pl.when(has_high)
+        def _():
+            for name in names:
+                for copy in halo_copies(name, True):
+                    copy.start()
+
+        @pl.when(has_low)
+        def _():
+            for name in names:
+                for copy in halo_copies(name, False):
+                    copy.start()
 
     def wait_halo(*names):
         @pl.when(has_low)
@@ -359,7 +366,10 @@
             done += n
 
     edge, chunks, edges = row_ranges(pairs)
-    wait("x", "band")
+    wait("band")
+    band_mid[pl.ds(0, span), lanes[0]] = band[:, lanes[2]]
+    band_mid[pl.ds(width, span), lanes[1]] = band[:, lanes[0]]
+    wait("x")
     pack(edge - 1, pairs - 2 * edge + 2)
     first_force(chunks[0])
     wait("t", "m")
@@ -388,28 +398,19 @@
 
     for k in range(1, inner):
         peak_copy(peak1, k, inner_id(k), 0).start()
-    @pl.when(has_high)
-    def _():
-        for name in "xtvme":
-            for copy in halo_copies(name, True):
-                copy.start()
-
-    @pl.when(has_low)
-    def _():
-        for name in "xtvme":
-            for copy in halo_copies(name, False):
-                copy.start()
-
+    start_halo("x", "t", "m")
     first_force(chunks[1])
-    wait("v")
+    wait("v", "e")
+    start_halo("v", "e")
     first_force(chunks[2])
     mix_rows(*chunks[0])
     mix_rows(*chunks[1])
-    wait_halo("x", "t", "v")
+    wait_halo("x")
     pack(-1, edge)
     pack(pairs - edge + 1, edge)
     first_force(*edges)
     mix_rows(*chunks[2])
+    wait_halo("t", "v")
     for first, n in edges:
         mix_rows(first, n)
 
@@ -424,11 +425,11 @@
     comp_of = pick_row // CODES
     code_of = pick_row % CODES
     picked = (pick_lane == comp_of * EDGE + code_of % EDGE) & (pick_lane < COMPS * EDGE)
-    found_table = jnp.zeros((COMPS * CODES, LOW), F32)
+    found = []
     for h in range(blocks):
         pick = jnp.where(picked & (code_of // EDGE == h), 1.0, 0.0).astype(BF16)
-        found_table += dot_t(pick, mixm[pl.ds(h * LOW, LOW), :])
-    table[...] = found_table.astype(BF16)
+        found.append(dot_t(pick, mixm[pl.ds(h * LOW, LOW), :]))
+    table[...] = (apart(p, sum(found[0::2])) + sum(found[1::2])).astype(BF16)
 
     def trace_copy(j):
         return pltpu.make_async_remote_copy(
@@ -460,9 +461,9 @@
                 )
         own[j] = result
         sent[j] = result.astype(BF16)
+    for j in (0, 2, 1):
         guarded(exists[j], lambda j=j: trace_copy(j).start())
 
-    wait("e")
     wait_halo("m", "e")
 
     def prepare(i, carry):
@@ -499,7 +500,7 @@
                     stack.append(jnp.where(mask, one, 0.0).astype(BF16))
                 stack.append(zero)
             sums.append(dot_t(hot[j, :, parts[q]], jnp.concatenate(stack, axis=0)))
-    summed = sum(sums[0::2]) + sum(sums[1::2])
+    summed = apart(p, sum(sums[0::2])) + sum(sums[1::2])
     both = summed[:, :LANES] + summed[:, LANES:]
     acc[...] = both
     first = both.astype(BF16)
@@ -569,36 +570,48 @@
 
     @pl.when(fine_group)
     def _():
-        done = 0
-        for first, n in chunks:
-            ready = blocks if first + n == chunks[-1][0] + chunks[-1][1] else (first + n) // half + 1
-            for h in range(done, ready):
-                finish(h)
-            done = ready
-            advance(pair_force(xb1, band, band_mid, (first, n)), (xo, wo), (xo, wo), ao, co, xb2, (first, n))
-
-    pl.when(fine_group & has_low)(lambda: far_copy(True).wait_recv())
-    pl.when(fine_group & has_high)(lambda: far_copy(False).wait_recv())
-    any_place = place[0]
-    for h in range(1, blocks):
-        any_place = any_place + place[h]
-    far = far_dst[...].reshape(2 * HALO, LANES)
-    far_first = far.astype(BF16)
-    far_pieces = jnp.concatenate([far_first, (far - far_first.astype(F32)).astype(BF16)], axis=1)
-    far_placed = dot(far_pieces, any_place)
-    seg_id = iota((SEG, width), 0)
-    for side, first_row in ((0, -HALO), (1, rows)):
-        for k in range(HALO):
-            j = (first_row + k + BASE) % seg_len
-            s = (first_row + k + BASE) // seg_len
-            at = (j // 2, j % 2)
-            one = far_placed[side * HALO + k : side * HALO + k + 1]
-            extra = square * three(dd[at]) * jnp.where(seg_id == s, one, 0.0)
-            there = xo[at] + extra
-            ao[at] = ao[at] + extra
-            wo[at] = wo[at] + extra
-            xo[at] = there
-            xb1[at[0] + 1, at[1]] = there.astype(BF16)
+        def sums_of(k):
+            return pair_force(xb1, band, band_mid, chunks[k])
+
+        def step_of(k, sums):
+            advance(sums, (xo, wo), (xo, wo), ao, co, xb2, chunks[k])
+
+        bounds = [(first + n) // half + 1 for first, n in chunks]
+        for h in range(1, bounds[0]):
+            finish(h)
+        sums = sums_of(0)
+        for h in range(bounds[0], bounds[1]):
+            finish(h)
+        step_of(0, sums)
+        sums = sums_of(1)
+        for h in [*range(bounds[1], blocks), 0]:
+            finish(h)
+        step_of(1, sums)
+        pl.when(has_low)(lambda: far_copy(True).wait_recv())
+        pl.when(has_high)(lambda: far_copy(False).wait_recv())
+        sums = sums_of(2)
+        any_place = place[0]
+        for h in range(1, blocks):
+            any_place = any_place + place[h]
+        far = far_dst[...].reshape(2 * HALO, LANES)
+        far_first = far.astype(BF16)
+        far_pieces = jnp.concatenate([far_first, (far - far_first.astype(F32)).astype(BF16)], axis=1)
+        far_placed = dot(far_pieces, any_place)
+        seg_id = iota((SEG, width), 0)
+        for side, first_row in ((0, -HALO), (1, rows)):
+            for k in range(HALO):
+                j = (first_row + k + BASE) % seg_len
+                s = (first_row + k + BASE) // seg_len
+                at = (j // 2, j % 2)
+                one = far_placed[side * HALO + k : side * HALO + k + 1]
+                extra = square * three(dd[at]) * jnp.where(seg_id == s, one, 0.0)
+                there = xo[at] + extra
+                ao[at] = ao[at] + extra
+                wo[at] = wo[at] + extra
+                xo[at] = there
+                xb1[at[0] + 1, at[1]] = there.astype(BF16)
+        step_of(2, sums)
+
     for par in range(2):
         xb1[0, par] = pltpu.roll(xo[pairs - 1, par], 1, 0).astype(BF16)
         xb1[pairs + 1, par] = pltpu.roll(xo[0, par], SEG - 1, 0).astype(BF16)
@@ -681,17 +694,17 @@
                 nxt[0, par] = pltpu.roll(xo[pairs - 1, par], 1, 0).astype(BF16)
                 nxt[pairs + 1, par] = pltpu.roll(xo[0, par], SEG - 1, 0).astype(BF16)
 
-        sums = pair_force(xb1, band, band_mid, *edges)
-        advance(sums, (x1, w1), (xo, wo), a, c, xb2, *edges)
-        xb2[middle] = mids[middle]
-        wrap(xb2)
-        for ranges in order:
+        def first_step(sums, ranges):
+            advance(sums, (x1, w1), (xo, wo), a, c, xb2, *ranges)
+            wrap(xb2)
+
+        def second_step(sums, ranges):
             src = (xo, wo) if ranges is edges else (x1, w1)
-            sums = pair_force(xb2, band, band_mid, *ranges)
             advance(sums, src, (xo, wo), a, c, xb3, *ranges)
-        wrap(xb3)
-        for ranges in order:
-            sums = pair_force(xb3, band, band_mid, *ranges)
+            if ranges is edges:
+                wrap(xb3)
+
+        def third_step(sums, ranges):
             done = 0
             for first, n in ranges:
                 for i in range(n):
@@ -700,6 +713,18 @@
                         w = wo[at] + a[at] - three(c[at]) * sums[par][done + i]
                         put(first + i, par, xo[at] + w, w)
                 done += n
+
+        tasks = [(first_step, xb1, edges)]
+        tasks += [(second_step, xb2, ranges) for ranges in order]
+        tasks += [(third_step, xb3, ranges) for ranges in order]
+        xb2[middle] = mids[middle]
+        last = None
+        for task, cur, ranges in tasks:
+            sums = pair_force(cur, band, band_mid, *ranges)
+            if last is not None:
+                last[0](*last[1:])
+            last = (task, sums, ranges)
+        last[0](*last[1:])
         drain()
 
 

time: 31.8 us -> 31.1 us (0.978)
  Pallas kernels: 30.9 us -> 30.2 us
    pallas_call x1, Pallas kernels: 19.6 us -> 19 us  [per_device(): pl.pallas_call(functools.partial(kernel, n_grp, n_patch), out_shape=[seg_...]
where the time goes in v3:
time: 31.1 us; the launch traced here: 31 us
  Pallas kernels  30.2 us (97%)
  between operations  0.8 us (3%)
    pallas_call x1, Pallas kernels, per_device(): pl.pallas_call(functools.partial(kernel, n_grp, n_patch), out_shape=[seg_...  19 us
    pallas_call x1, Pallas kernels, per_device(): pl.pallas_call(steps_kernel, out_shape=[jax.ShapeDtypeStruct(displace.sha...  11.2 us

profile of v3, /device:TPU:3, one launch (start us, length us, event | category | flops | bytes accessed | tf_op | source)
XLA Modules:
  0.0 31.0 jit_solution(1805895198669266849)
XLA Ops:
  0.6 19.0 %couple_step.1 = (f32[65,2,16,384]{3,2,1,0:T(8,128)S(1)}, f32[65,2,16,384]{3,2,1,0:T(8,128)S(1)}, f32[65,2,16,384]{3,2,1,0:T(8,128)S(1)}, f32[65,2,16,128]{3,2,1...) custom-call(f32[1,2048,384]{2,1,0:T(8,128)} %disp_hbm.1, ...), custom_call_target="tpu_custom_call" | custom-call | tf_op jit(solution)/shard_map/couple_step/pallas_call | solution.py:763
  19.6 11.2 %fine_steps.1 = (f32[1,2048,384]{2,1,0:T(8,128)}, f32[1,2048,384]{2,1,0:T(8,128)}) custom-call(f32[65,2,16,384]{3,2,1,0:T(8,128)S(1)} %get-tuple-element.11.x1, f32[65,2,16,384]{3,2,1,0:T(8,128)S(1)} %get-tuple-element.12.w1, f32[65,2,16,384]{3,2,1,0:T(8,128)S(1)} %get-tuple-element.13.a, f32[65,2,16,128]{3,2,1,0:T(8,128)S(1)} %get-tuple-element.14.c, ...), custom_call_target="tpu_custom_call" | custom-call | tf_op jit(solution)/shard_map/fine_steps/pallas_call | solution.py:819

commit v4 on v3

--- a/solution.py
+++ b/solution.py
@@ -657,7 +657,7 @@
                     at = pl.ds(OFF + j + half * 8 * seg_len, 8, stride=seg_len)
                     ref[c, at, :] = value[half * 8 : half * 8 + 8, c * LANES : (c + 1) * LANES]
 
-    def drain():
+    def whole():
         copies = []
         for k, (ref, out) in enumerate(((xs, disp_out), (vs, vel_out))):
             for c in range(COMPS):
@@ -668,10 +668,28 @@
                         out_sem.at[k, c],
                     )
                 )
+        return copies
+
+    def drain():
+        copies = whole()
         for copy in copies:
             copy.start()
         for copy in copies:
             copy.wait()
+
+    def pieces(bounds):
+        copies = []
+        for k, (ref, out) in enumerate(((xs, disp_out), (vs, vel_out))):
+            for lo, hi in bounds:
+                for c in range(COMPS):
+                    copies.append(
+                        pltpu.make_async_copy(
+                            ref.at[c, pl.ds(OFF + BASE + lo, hi - lo)],
+                            out.at[0, pl.ds(lo, hi - lo), pl.ds(c * LANES, LANES)],
+                            out_sem.at[k, c],
+                        )
+                    )
+        return copies
 
     @pl.when(g == 0)
     def _():
@@ -718,14 +736,26 @@
         tasks += [(second_step, xb2, ranges) for ranges in order]
         tasks += [(third_step, xb3, ranges) for ranges in order]
         xb2[middle] = mids[middle]
+        inner = []
+        begin, end = 2 * chunks[0][0], 2 * (chunks[-1][0] + chunks[-1][1])
+        for s in range(SEG):
+            lo = -(-(s * seg_len + begin - BASE) // 8) * 8
+            hi = (s * seg_len + end - BASE) // 8 * 8
+            inner.append((max(lo, 0), min(hi, rows)))
+        outer = [(lo, hi) for lo, hi in zip([0] + [hi for _, hi in inner], [lo for lo, _ in inner] + [rows]) if hi > lo]
         last = None
         for task, cur, ranges in tasks:
             sums = pair_force(cur, band, band_mid, *ranges)
             if last is not None:
                 last[0](*last[1:])
             last = (task, sums, ranges)
+        for copy in pieces(inner):
+            copy.start()
         last[0](*last[1:])
-        drain()
+        for copy in pieces(outer):
+            copy.start()
+        for copy in whole():
+            copy.wait()
 
 
 def per_device(

time: 31.1 us -> 30.3 us (0.974)
  Pallas kernels: 30.2 us -> 29.4 us
    pallas_call x1, Pallas kernels: 11.2 us -> 10.4 us  [per_device(): pl.pallas_call(steps_kernel, out_shape=[jax.ShapeDtypeStruct(displace.sha...]
where the time goes in v4:
time: 30.3 us; the launch traced here: 30.2 us
  Pallas kernels  29.4 us (97%)
  between operations  0.8 us (3%)
    pallas_call x1, Pallas kernels, per_device(): pl.pallas_call(functools.partial(kernel, n_grp, n_patch), out_shape=[seg_...  19 us
    pallas_call x1, Pallas kernels, per_device(): pl.pallas_call(steps_kernel, out_shape=[jax.ShapeDtypeStruct(displace.sha...  10.4 us

profile of v4, /device:TPU:3, one launch (start us, length us, event | category | flops | bytes accessed | tf_op | source)
XLA Modules:
  0.0 30.2 jit_solution(11786479779302455270)
XLA Ops:
  0.6 19.0 %couple_step.1 = (f32[65,2,16,384]{3,2,1,0:T(8,128)S(1)}, f32[65,2,16,384]{3,2,1,0:T(8,128)S(1)}, f32[65,2,16,384]{3,2,1,0:T(8,128)S(1)}, f32[65,2,16,128]{3,2,1...) custom-call(f32[1,2048,384]{2,1,0:T(8,128)} %disp_hbm.1, ...), custom_call_target="tpu_custom_call" | custom-call | tf_op jit(solution)/shard_map/couple_step/pallas_call | solution.py:793
  19.6 10.4 %fine_steps.1 = (f32[1,2048,384]{2,1,0:T(8,128)}, f32[1,2048,384]{2,1,0:T(8,128)}) custom-call(f32[65,2,16,384]{3,2,1,0:T(8,128)S(1)} %get-tuple-element.11.x1, f32[65,2,16,384]{3,2,1,0:T(8,128)S(1)} %get-tuple-element.12.w1, f32[65,2,16,384]{3,2,1,0:T(8,128)S(1)} %get-tuple-element.13.a, f32[65,2,16,128]{3,2,1,0:T(8,128)S(1)} %get-tuple-element.14.c, ...), custom_call_target="tpu_custom_call" | custom-call | tf_op jit(solution)/shard_map/fine_steps/pallas_call | solution.py:849
